TPU v7x, 1024 devices: a whole 4x4x32 slice. The times are simulated.
1024 devices in a mesh: gx: 16 (over x_hi, y, core), gy: 64 (over z, x_lo).
Axes of the slice: x: 4 (x_hi: 2, x_lo: 2; x = x_hi * 2 + x_lo), y: 4, z: 32, core: 2. Of those that a mesh axis runs over, the one named last changes fastest.
Arguments:
- conserved: float32 [5, 64, 1024, 128], P(None, 'gx', 'gy'), as said below
Outputs:
- increment: float32 [5, 64, 1024, 128], P(None, 'gx', 'gy')
- blending: float32 [16, 256, 32], P('gx', 'gy')
Inputs may be any that keep to these rules, and one draw needn't show every extreme that they name: `conserved`: every node's density and pressure are positive.
All inputs are finite; a program needn't handle non-finite values. Where the computation divides by a largest or mean magnitude, that divisor is 1e-20 or more.
Results may differ from a plain program's by a relative error of at most 0.0003.
Values sent between devices are 32-bit elements; how exact they have to be, the bound alone decides.
No kernel may reach another device: no remote copies, remote signals or barrier semaphores. Data moves between devices by JAX's collectives and lax.ppermute only.
A program may use at most 32 MiB of HBM per device.

v0:
```python
import math

import jax
import jax.numpy as jnp
import numpy as np
from jax import lax
from jax.experimental import pallas as pl
from jax.experimental.pallas import tpu as pltpu
from jax.sharding import Mesh
from jax.sharding import PartitionSpec as P


EVERY = ("gx", "gy")
SIZES = (2, 4, 2, 32, 2)

VMEM_BYTES = 6 << 20

WEIGHTS = (1.0 / 6.0, 5.0 / 6.0, 5.0 / 6.0, 1.0 / 6.0)


def tables():
    inverse_root = 1.0 / math.sqrt(5.0)
    points = np.array([-1.0, -inverse_root, inverse_root, 1.0])
    barycentric = np.array(
        [
            1.0 / np.prod([points[target] - points[other] for other in range(4) if other != target])
            for target in range(4)
        ]
    )
    derivative = np.zeros((4, 4))
    for target in range(4):
        for source in range(4):
            if target != source:
                derivative[target, source] = (
                    barycentric[source] / barycentric[target] / (points[target] - points[source])
                )
    legendre = np.stack(
        [np.ones(4), points, (3.0 * points**2 - 1.0) / 2.0, (5.0 * points**3 - 3.0 * points) / 2.0],
        1,
    )
    legendre = legendre * np.sqrt(np.arange(4) + 0.5)
    weight_column = np.array(WEIGHTS)[:, None]
    discrete_norms = np.sum(weight_column * legendre * legendre, 0)
    inverse = (weight_column * legendre).T / discrete_norms[:, None]
    return derivative, inverse


DERIVATIVE, INVERSE = tables()
SPLIT = [[2.0 * WEIGHTS[k] * float(DERIVATIVE[k, j]) for j in range(4)] for k in range(4)]


def roll(value, shift, axis):
    size = value.shape[axis]
    return pltpu.roll(value, shift % size, axis)


def local_node(shape, axis):
    return lax.broadcasted_iota(jnp.int32, shape, axis) % 4


def by_node(node, values):
    out = jnp.full(node.shape, values[3], jnp.float32)
    for k in range(3):
        out = jnp.where(node == k, jnp.float32(values[k]), out)
    return out


def primitives(parts):
    density = parts[0]
    inverse = 1.0 / density
    velocity = [parts[1 + d] * inverse for d in range(3)]
    square = velocity[0] * velocity[0] + velocity[1] * velocity[1] + velocity[2] * velocity[2]
    pressure = 0.4 * (parts[4] - 0.5 * density * square)
    return density, velocity, pressure, inverse


def sound_of(pressure, inverse):
    return jnp.sqrt(1.4 * pressure * inverse)


NAMES = ("r", "u", "v", "w", "p", "c", "s", "lr", "ls", "m1", "m2", "m3", "e")


def full_state(parts):
    density, velocity, pressure, inverse = primitives(parts)
    ratio = density / pressure
    return {
        "r": density,
        "u": velocity[0],
        "v": velocity[1],
        "w": velocity[2],
        "p": pressure,
        "c": sound_of(pressure, inverse),
        "s": ratio,
        "lr": jnp.log(density),
        "ls": jnp.log(ratio),
        "m1": parts[1],
        "m2": parts[2],
        "m3": parts[3],
        "e": parts[4],
    }


def mean_parts(a, b, log_a, log_b):
    total = a + b
    gap = a - b
    relative = gap / total
    square = relative * relative
    small = square < 0.01
    series = 1.0 + square * (1.0 / 3.0 + square * (1.0 / 5.0 + square * (1.0 / 7.0)))
    top = jnp.where(small, 0.5 * total, gap)
    bottom = jnp.where(small, series, log_a - log_b)
    return top, bottom


def pair_flux(a, b, normal):
    top, bottom = mean_parts(a["r"], b["r"], a["lr"], b["lr"])
    mass = top / bottom
    top, bottom = mean_parts(a["s"], b["s"], a["ls"], b["ls"])
    inverse_beta = bottom / top
    key = "uvw"[normal]
    flux0 = mass * (0.5 * (a[key] + b[key]))
    out = [flux0]
    for other in range(3):
        name = "uvw"[other]
        term = flux0 * (0.5 * (a[name] + b[name]))
        if other == normal:
            term = term + 0.5 * (a["p"] + b["p"])
        out.append(term)
    dot = 0.5 * (a["u"] * b["u"] + a["v"] * b["v"] + a["w"] * b["w"])
    out.append(
        flux0 * (dot + 2.5 * inverse_beta) + 0.5 * (a["p"] * b[key] + b["p"] * a[key])
    )
    return out


def dissipation(a, b, normal):
    key = "uvw"[normal]
    half = 0.5 * jnp.maximum(jnp.abs(a[key]) + a["c"], jnp.abs(b[key]) + b["c"])
    return [half * (b[q] - a[q]) for q in ("r", "m1", "m2", "m3", "e")]


def forward_kernel(in_ref, out_ref):
    row = jnp.max(in_ref[...], axis=0, keepdims=True)
    out_ref[...] = jnp.broadcast_to(row, out_ref.shape)


def transform(value, axis):
    node = local_node(value.shape, axis)
    total = None
    for offset in range(-3, 4):
        coefficients = [
            float(INVERSE[a, a + offset]) if 0 <= a + offset < 4 else 0.0 for a in range(4)
        ]
        shifted = value if offset == 0 else roll(value, -offset, axis)
        term = by_node(node, coefficients) * shifted
        total = term if total is None else total + term
    return total


def spread_sum(value, axis):
    index = lax.broadcasted_iota(jnp.int32, value.shape, axis)
    for step in (1, 2):
        other = jnp.where((index // step) % 2 == 1, roll(value, step, axis), roll(value, -step, axis))
        value = value + other
    return value


def raw_blending(layers):
    indicated = []
    for parts in layers:
        density, _, pressure, _ = primitives(parts)
        indicated.append(density * pressure)
    shape = indicated[0].shape
    node_y, node_z = local_node(shape, 0), local_node(shape, 1)
    degree = jnp.maximum(node_y, node_z)
    high = mid = low = None
    zero = jnp.zeros(shape, jnp.float32)
    for a in range(4):
        modes = sum(float(INVERSE[a, k]) * indicated[k] for k in range(4))
        modes = transform(transform(modes, 0), 1)
        square = modes * modes
        if a == 3:
            high = high + square
            continue
        top = jnp.where(degree == 3, square, zero)
        high = top if high is None else high + top
        if a == 2:
            mid = mid + jnp.where(degree < 3, square, zero)
            continue
        middle = jnp.where(degree == 2, square, zero)
        mid = middle if mid is None else mid + middle
        rest = jnp.where(degree < 2, square, zero)
        low = rest if low is None else low + rest
    high, mid, low = (spread_sum(spread_sum(v, 0), 1) for v in (high, mid, low))
    three = low + mid
    energy = jnp.maximum(high / (three + high + 1e-06), mid / (three + 1e-06))
    threshold = 0.5 * 10.0 ** (-1.8 * 4.0**0.25)
    sharpness = math.log(9999.0)
    raw = 1.0 / (1.0 + jnp.exp(-(sharpness / threshold) * (energy - threshold)))
    return jnp.minimum(raw, 0.5)


FIRST_X, MIDDLE_X = 5, 9
MIDDLE_Y = 9
OWN_Y = 9
X_TURN = 10


def x_slot(place, plane, own_ring):
    b_pair = place % 2 == 1
    if own_ring:
        if place == GX_SIZE - 1:
            return "Q"
        if place == 0:
            return "S"
        if place == X_TURN:
            return "R"
        return "P" if b_pair == (place < X_TURN) else "Q"
    if plane >= MIDDLE_X:
        return "Q" if b_pair else "R"
    return "P" if b_pair == (plane < FIRST_X) else "Q"


def y_slot(place, own_ring):
    b_pair, plane = place % 2 == 1, place // 2
    if own_ring:
        if plane < OWN_Y:
            if b_pair:
                return "R" if plane == OWN_Y - 1 else "P"
            return "Q"
        if plane >= MIDDLE_Y or (b_pair and plane == MIDDLE_Y - 1):
            return "R" if b_pair else "Q"
    if b_pair:
        return "Q"
    return "P" if plane < MIDDLE_Y else "R"


def sides():
    gx, gy = lax.axis_index("gx"), lax.axis_index("gy")
    core, plane, xl = gx & 1, gy >> 1, gy & 1
    first = plane < FIRST_X
    own_x = gy == 0
    turned = jnp.logical_or(gx == 0, gx > X_TURN)
    own_turned = jnp.logical_and(own_x, turned)
    own_straight = jnp.logical_and(own_x, jnp.logical_not(turned))
    middle = jnp.logical_and(plane >= FIRST_X, plane < MIDDLE_X)
    a_in_p = jnp.logical_or(middle, own_turned)
    a_in_q = jnp.logical_or(jnp.logical_and(first, jnp.logical_not(own_turned)), own_straight)
    own_y = gx == 0
    near = plane < OWN_Y
    b_in_p_y = jnp.logical_and(own_y, near)
    a_in_q_y = jnp.logical_and(own_y, jnp.logical_or(near, plane >= MIDDLE_Y))

    def side(a_pair, parity):
        return jnp.where(a_pair, 1 - parity, parity)

    along_x = [side(a_in_p, core), side(a_in_q, core), 1 - core]
    along_y = [
        side(jnp.logical_not(b_in_p_y), xl),
        side(a_in_q_y, xl),
        side(jnp.logical_not(own_y), xl),
    ]
    return along_x, along_y


def first_kernel(conserved_hbm, rows_hbm, raw_ref, xp, xq, xr, yp, yq, yr, held_ref, rows_ref, sems):
    copies = [
        pltpu.make_async_copy(conserved_hbm.at[:, x], held_ref.at[:, x], sems.at[x]) for x in range(4)
    ]
    for copy in copies:
        copy.start()
    best = None
    for x in range(4):
        copies[x].wait()
        _, velocity, pressure, inverse = primitives([held_ref[q, x] for q in range(5)])
        speed = (
            jnp.abs(velocity[0])
            + jnp.abs(velocity[1])
            + jnp.abs(velocity[2])
            + 3.0 * sound_of(pressure, inverse)
        )
        best = speed if best is None else jnp.maximum(best, speed)
    row = jnp.max(best, axis=0, keepdims=True)
    rows_ref[...] = jnp.broadcast_to(row[None], rows_ref.shape)
    sent = pltpu.make_async_copy(rows_ref, rows_hbm, sems.at[4])
    sent.start()
    raw = raw_blending([[held_ref[q, x] for q in range(5)] for x in range(4)])
    raw_ref[...] = raw

    def put_x(face_ref, x):
        for q in range(5):
            face_ref[q] = held_ref[q, x]
        face_ref[5] = raw

    def put_y(face_ref, row):
        for q in range(5):
            for x in range(4):
                face_ref[q, x : x + 1] = held_ref[q, x, row : row + 1]
        face_ref[5] = jnp.broadcast_to(raw[row : row + 1], (4, 128))

    def fill(side, put, face_ref, low, high):
        pl.when(side == 0)(lambda: put(face_ref, low))
        pl.when(side == 1)(lambda: put(face_ref, high))

    along_x, along_y = sides()
    for side, face_ref in zip(along_x, (xp, xq, xr), strict=True):
        fill(side, put_x, face_ref, 0, 3)
    for side, face_ref in zip(along_y, (yp, yq, yr), strict=True):
        fill(side, put_y, face_ref, 0, 15)
    sent.wait()


def physics_kernel(
    conserved_ref,
    raw_ref,
    xp,
    xq,
    xr,
    yp,
    yq,
    yr,
    xs,
    out_ref,
    blend_hbm,
    blend_ref,
    sem,
    state_ref,
    xprev_ref,
    xnext_ref,
    yprev_ref,
    ynext_ref,
):
    along_x, along_y = sides()
    for flags, refs, prev_ref, next_ref in (
        (along_x + along_x[2:], (xp, xq, xr, xs), xprev_ref, xnext_ref),
        (along_y, (yp, yq, yr), yprev_ref, ynext_ref),
    ):
        low = high = None
        for flag, ref in zip(flags, refs, strict=True):
            value = ref[...]
            up = flag.astype(jnp.float32)
            above, below = value * up, value * (1.0 - up)
            low = below if low is None else low + below
            high = above if high is None else high + above
        prev_ref[...] = low
        next_ref[...] = high

    raw = raw_ref[...]
    shape = raw.shape
    row = lax.broadcasted_iota(jnp.int32, shape, 0)
    node_y, node_z = row % 4, local_node(shape, 1)

    before = jnp.where(row < 4, jnp.broadcast_to(yprev_ref[5, 0:1], shape), roll(raw, 4, 0))
    after = jnp.where(row >= 12, jnp.broadcast_to(ynext_ref[5, 0:1], shape), roll(raw, -4, 0))
    around = jnp.maximum(xprev_ref[5], xnext_ref[5])
    around = jnp.maximum(around, jnp.maximum(before, after))
    around = jnp.maximum(around, jnp.maximum(roll(raw, 4, 1), roll(raw, -4, 1)))
    blend = jnp.maximum(raw, 0.5 * around)
    pick_z = (
        lax.broadcasted_iota(jnp.int32, (128, 32), 0) == 4 * lax.broadcasted_iota(jnp.int32, (128, 32), 1)
    ).astype(jnp.float32)
    compact = jnp.dot(
        blend, pick_z, precision=lax.Precision.HIGHEST, preferred_element_type=jnp.float32
    )
    for element in range(4):
        blend_ref[0, element : element + 1] = compact[4 * element : 4 * element + 1]
    sent = pltpu.make_async_copy(blend_ref, blend_hbm, sem)
    sent.start()
    keep = 1.0 - blend

    for x in range(4):
        state = full_state([conserved_ref[q, x] for q in range(5)])
        for i, name in enumerate(NAMES[:9]):
            state_ref[i, x] = state[name]

    def load(x):
        state = {name: state_ref[i, x] for i, name in enumerate(NAMES[:9])}
        for i, name in enumerate(NAMES[9:]):
            state[name] = conserved_ref[1 + i, x]
        return state

    def store(x, values, first=False):
        for q in range(5):
            out_ref[q, x] = values[q] if first else out_ref[q, x] + values[q]

    y_prev = full_state([yprev_ref[q] for q in range(5)])
    y_next = full_state([ynext_ref[q] for q in range(5)])
    edge = {}
    for i, name in enumerate(NAMES[:9]):
        edge[name] = jnp.concatenate([state_ref[i, x, 0:1] for x in range(4)], axis=0)
    for i, name in enumerate(NAMES[9:]):
        edge[name] = jnp.concatenate([conserved_ref[1 + i, x, 0:1] for x in range(4)], axis=0)
    low_face = [
        f - d for f, d in zip(pair_flux(y_prev, edge, 1), dissipation(y_prev, edge, 1), strict=True)
    ]

    def along(axis, node, x, state):
        normal = axis + 1
        one = jnp.ones(shape, jnp.float32)
        step = [SPLIT[0][1], SPLIT[1][2], SPLIT[2][3], 0.0]
        inner = node < 3
        weight_f = jnp.where(inner, keep * by_node(node, step) + blend, one)
        weight_d = jnp.where(inner, blend, one)
        weight_far = keep * by_node(node, [SPLIT[0][2], SPLIT[1][3], 0.0, SPLIT[3][0]])
        next_ = {}
        for name in NAMES:
            moved = roll(state[name], -1, axis)
            if axis == 0:
                moved = jnp.where(row == 15, jnp.broadcast_to(y_next[name][x : x + 1], shape), moved)
            next_[name] = moved
        flux = pair_flux(state, next_, normal)
        loss = dissipation(state, next_, normal)
        far = {
            name: jnp.where(node == 3, roll(state[name], 3, axis), roll(state[name], -2, axis))
            for name in ("r", "u", "v", "w", "p", "s", "lr", "ls")
        }
        cross = pair_flux(state, far, normal)
        inverse_weight = by_node(node, [-1.0 / w for w in WEIGHTS])
        out = []
        for q in range(5):
            near = weight_f * flux[q] - weight_d * loss[q]
            back = roll(near, 1, axis)
            if axis == 0:
                back = jnp.where(row == 0, jnp.broadcast_to(low_face[q][x : x + 1], shape), back)
            wide = weight_far * cross[q]
            taken = jnp.where(node >= 2, roll(wide, 2, axis), jnp.where(node == 0, roll(wide, -3, axis), 0.0))
            out.append(inverse_weight * (near - back + wide - taken))
        return out

    for x in range(4):
        state = load(x)
        in_y = along(0, node_y, x, state)
        in_z = along(1, node_z, x, state)
        store(x, [a + b for a, b in zip(in_y, in_z, strict=True)], first=True)

    def gather(other):
        return full_state([other[q] for q in range(5)])

    for first in range(4):
        for second in range(first + 1, 4):
            a, b = load(first), load(second)
            flux = pair_flux(a, b, 0)
            if second == first + 1:
                weight = keep * SPLIT[first][second] + blend
                loss = dissipation(a, b, 0)
                term = [weight * f - blend * d for f, d in zip(flux, loss, strict=True)]
            else:
                weight = keep * SPLIT[first][second]
                term = [weight * f for f in flux]
            store(first, [(-1.0 / WEIGHTS[first]) * t for t in term])
            store(second, [(1.0 / WEIGHTS[second]) * t for t in term])
    a, b = gather(xprev_ref), load(0)
    flux, loss = pair_flux(a, b, 0), dissipation(a, b, 0)
    store(0, [(1.0 / WEIGHTS[0]) * (f - d) for f, d in zip(flux, loss, strict=True)])
    a, b = load(3), gather(xnext_ref)
    flux, loss = pair_flux(a, b, 0), dissipation(a, b, 0)
    store(3, [(-1.0 / WEIGHTS[3]) * (f - d) for f, d in zip(flux, loss, strict=True)])
    sent.wait()


def scale_kernel(tendency_ref, speed_ref, out_ref):
    row = jnp.max(speed_ref[...], axis=0)
    top = jnp.max(row, axis=1, keepdims=True)
    step = 0.25 / top
    for q in range(5):
        for x in range(4):
            out_ref[q, x] = tendency_ref[q, x] * step


def call(kernel, outs, *args, scratch=(), **kwargs):
    return pl.pallas_call(
        kernel,
        out_shape=[jax.ShapeDtypeStruct(shape, jnp.float32) for shape in outs],
        scratch_shapes=list(scratch),
        compiler_params=pltpu.CompilerParams(vmem_limit_bytes=VMEM_BYTES),
        **kwargs,
    )(*args)


DEVICES = np.arange(math.prod(SIZES)).reshape(SIZES)
COUNT = DEVICES.size
GX_SIZE, GY_SIZE = math.prod(SIZES[:3]), math.prod(SIZES[3:])
Z_SIZE = SIZES[3]
Z_LEAD = 22
CHAIN_FACES = ("xP", "xQ", "xR", "yP", "yQ", "yR", "xS")


def trade(block, along_x, slot):
    grid = DEVICES.reshape(GX_SIZE, GY_SIZE)
    pairs = []
    if along_x:
        for place in range(GX_SIZE):
            for ring in range(GY_SIZE):
                if x_slot(place, ring // SIZES[4], ring == 0) == slot:
                    pairs.append((int(grid[place, ring]), int(grid[(place + 1) % GX_SIZE, ring])))
    else:
        for place in range(GY_SIZE):
            for ring in range(GX_SIZE):
                if y_slot(place, ring == 0) == slot:
                    pairs.append((int(grid[ring, place]), int(grid[ring, (place + 1) % GY_SIZE])))
    pairs += [(b, a) for a, b in pairs]
    return lax.ppermute(block, EVERY, pairs)


def z_groups():
    order = [Z_LEAD] + [z for z in range(Z_SIZE) if z != Z_LEAD]
    return DEVICES.transpose(0, 1, 2, 4, 3)[..., order].reshape(-1, Z_SIZE).tolist()


def plane_groups():
    index = DEVICES.transpose(3, 0, 1, 2, 4).reshape(Z_SIZE, -1)
    sizes = SIZES[:3] + SIZES[4:]
    lead = int(np.ravel_multi_index((sizes[0] - 1, sizes[1] // 2, 1, 0), sizes))
    order = [lead] + [i for i in range(index.shape[1]) if i != lead]
    return index[:, order].tolist()


def exchange(rows, groups):
    return lax.all_to_all(rows, EVERY, 0, 0, axis_index_groups=groups)


def body(conserved):
    plane = COUNT // Z_SIZE
    x_face, y_face = (6, 16, 128), (6, 4, 128)
    rows, raw, *faces = call(
        first_kernel,
        [(Z_SIZE, 1, 128), (16, 128)] + [x_face] * 3 + [y_face] * 3,
        pltpu.with_memory_space_constraint(conserved, pltpu.HBM),
        scratch=[
            pltpu.VMEM((5, 4, 16, 128), jnp.float32),
            pltpu.VMEM((Z_SIZE, 1, 128), jnp.float32),
            pltpu.SemaphoreType.DMA((5,)),
        ],
        in_specs=[pl.BlockSpec(memory_space=pltpu.HBM)],
        out_specs=[pl.BlockSpec(memory_space=pltpu.HBM)]
        + [pl.BlockSpec(memory_space=pltpu.VMEM)] * 7,
    )
    got = {}

    def swap(*names):
        for name in names:
            i = CHAIN_FACES.index("xR" if name == "xS" else name)
            got[name] = trade(faces[i], name[0] == "x", name[1])

    swap("xP", "yP")
    column = exchange(rows, z_groups())
    swap("xS", "xQ", "yQ", "xR")
    (forward,) = call(forward_kernel, [(plane, 1, 128)], column)
    speeds = exchange(forward, plane_groups())
    swap("yR")
    tendency, blending = call(
        physics_kernel,
        [(5, 4, 16, 128), (1, 4, 32)],
        conserved,
        raw,
        *(got[name] for name in CHAIN_FACES),
        out_specs=[pl.BlockSpec(memory_space=pltpu.VMEM), pl.BlockSpec(memory_space=pltpu.HBM)],
        scratch=[
            pltpu.VMEM((1, 4, 32), jnp.float32),
            pltpu.SemaphoreType.DMA,
            pltpu.VMEM((9, 4, 16, 128), jnp.float32),
            pltpu.VMEM(x_face, jnp.float32),
            pltpu.VMEM(x_face, jnp.float32),
            pltpu.VMEM(y_face, jnp.float32),
            pltpu.VMEM(y_face, jnp.float32),
        ],
    )
    (increment,) = call(scale_kernel, [(5, 4, 16, 128)], tendency, speeds)
    return increment, blending


def solution(mesh):
    split = Mesh(mesh.devices.reshape(GX_SIZE, GY_SIZE), EVERY)
    return jax.shard_map(
        body,
        mesh=split,
        in_specs=(P(None, "gx", "gy", None),),
        out_specs=(P(None, "gx", "gy", None), P("gx", "gy", None)),
        check_vma=False,
    )
```

profile of v0, /device:TPU:1, one launch (start us, length us, event | category | flops | bytes accessed | tf_op | source)
XLA Modules:
  0.0 62.1 jit_solution(17785781724161751182)
XLA Ops:
  0.6 0.0 copy-start
  0.6 1.8 %shard_map.30 = (f32[32,1,128]{2,1,0:T(1,128)}, f32[16,128]{1,0:T(8,128)S(1)}, f32[6,16,128]{2,1,0:T(8,128)S(1)}, f32[6,16,128]{2,1,0:T(8,128)S(1)}, f32[6,16,12...) custom-call(f32[5,4,16,128]{3,2,1,0:T(8,128)} %conserved_ref.1), custom_call_target="tpu_custom_call" | custom-call | tf_op jit(solution)/shard_map/pallas_call | solution.py:472
  2.5 29.5 %all-to-all-start = ((f32[32,1,128]{2,1,0:T(1,128)}), f32[32,1,128]{2,1,0:T(1,128)S(1)}, u32[]{:S(2)}, u32[]{:S(2)}) async-start(f32[32,1,128]{2,1,0:T(1,128)} %get-tuple-element.20), calls=%async_computation | async-start | bytes 32768 | tf_op jit(solution)/shard_map/all_to_all | solution.py:520
  32.0 4.3 %collective-permute-start = (f32[6,16,128]{2,1,0:T(8,128)S(1)}, f32[6,16,128]{2,1,0:T(8,128)S(1)}, u32[]{:S(2)}, u32[]{:S(2)}) collective-permute-start(f32[6,16,128]{2,1,0:T(8,128)S(1)} %get-tuple-element.13), channel_id=1, source_target_pairs={{10,74},{11,75},{12,76},{13,77},{14,78},{15,79},{16,80},{17,81},{6... | collective-permute-start | bytes 147464 | tf_op jit(solution)/shard_map/ppermute | solution.py:503
  36.4 0.7 %collective-permute-start.1 = (f32[6,16,128]{2,1,0:T(8,128)S(1)}, f32[6,16,128]{2,1,0:T(8,128)S(1)}, u32[]{:S(2)}, u32[]{:S(2)}) collective-permute-start(f32[6,16,128]{2,1,0:T(8,128)S(1)} %get-tuple-element.14), channel_id=1, source_target_pairs={{1,65},{2,66},{3,67},{4,68},{5,69},{6,70},{7,71},{8,72},{9,73},{74... | collective-permute-start | bytes 147464 | tf_op jit(solution)/shard_map/ppermute | solution.py:503
  37.1 7.6 %collective-permute-start.6 = (f32[6,16,128]{2,1,0:T(8,128)S(1)}, f32[6,16,128]{2,1,0:T(8,128)S(1)}, u32[]{:S(2)}, u32[]{:S(2)}) collective-permute-start(f32[6,16,128]{2,1,0:T(8,128)S(1)} %get-tuple-element.15), channel_id=1, source_target_pairs={{0,64},{64,0}} | collective-permute-start | bytes 147464 | tf_op jit(solution)/shard_map/ppermute | solution.py:503
  44.6 0.7 %collective-permute-start.2 = (f32[6,16,128]{2,1,0:T(8,128)S(1)}, f32[6,16,128]{2,1,0:T(8,128)S(1)}, u32[]{:S(2)}, u32[]{:S(2)}) collective-permute-start(f32[6,16,128]{2,1,0:T(8,128)S(1)} %get-tuple-element.15), channel_id=1, source_target_pairs={{18,82},{19,83},{20,84},{21,85},{22,86},{23,87},{24,88},{25,89},{2... | collective-permute-start | bytes 147464 | tf_op jit(solution)/shard_map/ppermute | solution.py:503
  45.3 1.9 %collective-permute-start.3 = (f32[6,4,128]{2,1,0:T(4,128)S(1)}, f32[6,4,128]{2,1,0:T(4,128)S(1)}, u32[]{:S(2)}, u32[]{:S(2)}) collective-permute-start(f32[6,4,128]{2,1,0:T(4,128)S(1)} %get-tuple-element.16), channel_id=1, source_target_pairs={{64,65},{128,129},{192,193},{256,257},{320,321},{384,385},{448,449... | collective-permute-start | bytes 36872 | tf_op jit(solution)/shard_map/ppermute | solution.py:503
  47.2 2.5 %collective-permute-done.3.yp = f32[6,4,128]{2,1,0:T(4,128)S(1)} collective-permute-done((f32[6,4,128]{2,1,0:T(4,128)S(1)}, f32[6,4,128]{2,1,0:T(4,128)S(1)}, u32[]{:S(2)}, u32[]{:S(2)}) %collective-permute-start.3) | collective-permute-done | bytes 12320 | tf_op jit(solution)/shard_map/ppermute | solution.py:503
  49.7 1.9 %collective-permute-start.4 = (f32[6,4,128]{2,1,0:T(4,128)S(1)}, f32[6,4,128]{2,1,0:T(4,128)S(1)}, u32[]{:S(2)}, u32[]{:S(2)}) collective-permute-start(f32[6,4,128]{2,1,0:T(4,128)S(1)} %get-tuple-element.17), channel_id=1, source_target_pairs={{0,1},{65,66},{129,130},{193,194},{257,258},{321,322},{385,386},{4... | collective-permute-start | bytes 36872 | tf_op jit(solution)/shard_map/ppermute | solution.py:503
  51.6 0.0 all-to-all-done.in_ref
  51.7 0.6 %shard_map.32 = f32[32,1,128]{2,1,0:T(1,128)} custom-call(f32[32,1,128]{2,1,0:T(1,128)S(1)} %all-to-all-done.in_ref), custom_call_target="tpu_custom_call" | custom-call | tf_op jit(solution)/shard_map/pallas_call | solution.py:472
  52.3 6.8 %all-to-all-start.1 = ((f32[32,1,128]{2,1,0:T(1,128)}), f32[32,1,128]{2,1,0:T(1,128)S(1)}, u32[]{:S(2)}, u32[]{:S(2)}) async-start(f32[32,1,128]{2,1,0:T(1,128)} %shard_map.32), calls=%async_computation.1 | async-start | bytes 32768 | tf_op jit(solution)/shard_map/all_to_all | solution.py:520
  59.1 0.0 collective-permute-done.4.yq
  59.2 0.7 %collective-permute-start.5 = (f32[6,4,128]{2,1,0:T(4,128)S(1)}, f32[6,4,128]{2,1,0:T(4,128)S(1)}, u32[]{:S(2)}, u32[]{:S(2)}) collective-permute-start(f32[6,4,128]{2,1,0:T(4,128)S(1)} %get-tuple-element.18), channel_id=1, source_target_pairs={{17,18},{82,83},{146,147},{210,211},{274,275},{338,339},{402,403},... | collective-permute-start | bytes 36872 | tf_op jit(solution)/shard_map/ppermute | solution.py:503
  59.8 0.0 collective-permute-done.5.yr
  59.8 0.0 collective-permute-done.xp
  59.8 0.0 collective-permute-done.1.xq
  59.9 0.0 collective-permute-done.6.xs
  59.9 0.0 collective-permute-done.2.xr
  59.9 0.0 copy-done
  59.9 1.5 %shard_map.31 = (f32[5,4,16,128]{3,2,1,0:T(8,128)S(1)}, f32[1,4,32]{2,1,0:T(4,128)}) custom-call(f32[5,4,16,128]{3,2,1,0:T(8,128)S(1)} %copy-done, f32[16,128]{1,0:T(8,128)S(1)} %get-tuple-element.12.raw_ref, f32[6,16,128]{2,1,0:T(8,128)S(1)} %collective-permute-done.xp, f32[6,16,128]{2,1,0:T(8,128)S(1)} %collective-permute-done.1.xq, ...), custom_call_target="tpu_custom_call" | custom-call | tf_op jit(solution)/shard_map/pallas_call | solution.py:472
  61.4 0.0 all-to-all-done.1.speed_ref
  61.4 0.8 %shard_map.33 = f32[5,4,16,128]{3,2,1,0:T(8,128)} custom-call(f32[5,4,16,128]{3,2,1,0:T(8,128)S(1)} %get-tuple-element.19.tendency_ref, f32[32,1,128]{2,1,0:T(1,128)S(1)} %all-to-all-done.1.speed_ref), custom_call_target="tpu_custom_call" | custom-call | tf_op jit(solution)/shard_map/pallas_call | solution.py:472
Async XLA Ops:
  0.6 59.2 %copy-start = (f32[5,4,16,128]{3,2,1,0:T(8,128)S(1)}, f32[5,4,16,128]{3,2,1,0:T(8,128)}, u32[]{:S(2)}) copy-start(f32[5,4,16,128]{3,2,1,0:T(8,128)} %conserved_ref.1) | copy-start | bytes 491524
  2.5 49.2 %all-to-all-start = ((f32[32,1,128]{2,1,0:T(1,128)}), f32[32,1,128]{2,1,0:T(1,128)S(1)}, u32[]{:S(2)}, u32[]{:S(2)}) async-start(f32[32,1,128]{2,1,0:T(1,128)} %get-tuple-element.20), calls=%async_computation | async-start | bytes 32768 | tf_op jit(solution)/shard_map/all_to_all | solution.py:520
  32.0 27.8 %collective-permute-start = (f32[6,16,128]{2,1,0:T(8,128)S(1)}, f32[6,16,128]{2,1,0:T(8,128)S(1)}, u32[]{:S(2)}, u32[]{:S(2)}) collective-permute-start(f32[6,16,128]{2,1,0:T(8,128)S(1)} %get-tuple-element.13), channel_id=1, source_target_pairs={{10,74},{11,75},{12,76},{13,77},{14,78},{15,79},{16,80},{17,81},{6... | collective-permute-start | bytes 147464 | tf_op jit(solution)/shard_map/ppermute | solution.py:503
  36.4 23.5 %collective-permute-start.1 = (f32[6,16,128]{2,1,0:T(8,128)S(1)}, f32[6,16,128]{2,1,0:T(8,128)S(1)}, u32[]{:S(2)}, u32[]{:S(2)}) collective-permute-start(f32[6,16,128]{2,1,0:T(8,128)S(1)} %get-tuple-element.14), channel_id=1, source_target_pairs={{1,65},{2,66},{3,67},{4,68},{5,69},{6,70},{7,71},{8,72},{9,73},{74... | collective-permute-start | bytes 147464 | tf_op jit(solution)/shard_map/ppermute | solution.py:503
  37.1 22.8 %collective-permute-start.6 = (f32[6,16,128]{2,1,0:T(8,128)S(1)}, f32[6,16,128]{2,1,0:T(8,128)S(1)}, u32[]{:S(2)}, u32[]{:S(2)}) collective-permute-start(f32[6,16,128]{2,1,0:T(8,128)S(1)} %get-tuple-element.15), channel_id=1, source_target_pairs={{0,64},{64,0}} | collective-permute-start | bytes 147464 | tf_op jit(solution)/shard_map/ppermute | solution.py:503
  44.6 15.2 %collective-permute-start.2 = (f32[6,16,128]{2,1,0:T(8,128)S(1)}, f32[6,16,128]{2,1,0:T(8,128)S(1)}, u32[]{:S(2)}, u32[]{:S(2)}) collective-permute-start(f32[6,16,128]{2,1,0:T(8,128)S(1)} %get-tuple-element.15), channel_id=1, source_target_pairs={{18,82},{19,83},{20,84},{21,85},{22,86},{23,87},{24,88},{25,89},{2... | collective-permute-start | bytes 147464 | tf_op jit(solution)/shard_map/ppermute | solution.py:503
  45.3 4.4 %collective-permute-start.3 = (f32[6,4,128]{2,1,0:T(4,128)S(1)}, f32[6,4,128]{2,1,0:T(4,128)S(1)}, u32[]{:S(2)}, u32[]{:S(2)}) collective-permute-start(f32[6,4,128]{2,1,0:T(4,128)S(1)} %get-tuple-element.16), channel_id=1, source_target_pairs={{64,65},{128,129},{192,193},{256,257},{320,321},{384,385},{448,449... | collective-permute-start | bytes 36872 | tf_op jit(solution)/shard_map/ppermute | solution.py:503
  49.7 9.4 %collective-permute-start.4 = (f32[6,4,128]{2,1,0:T(4,128)S(1)}, f32[6,4,128]{2,1,0:T(4,128)S(1)}, u32[]{:S(2)}, u32[]{:S(2)}) collective-permute-start(f32[6,4,128]{2,1,0:T(4,128)S(1)} %get-tuple-element.17), channel_id=1, source_target_pairs={{0,1},{65,66},{129,130},{193,194},{257,258},{321,322},{385,386},{4... | collective-permute-start | bytes 36872 | tf_op jit(solution)/shard_map/ppermute | solution.py:503
  52.3 9.1 %all-to-all-start.1 = ((f32[32,1,128]{2,1,0:T(1,128)}), f32[32,1,128]{2,1,0:T(1,128)S(1)}, u32[]{:S(2)}, u32[]{:S(2)}) async-start(f32[32,1,128]{2,1,0:T(1,128)} %shard_map.32), calls=%async_computation.1 | async-start | bytes 32768 | tf_op jit(solution)/shard_map/all_to_all | solution.py:520
  59.2 0.7 %collective-permute-start.5 = (f32[6,4,128]{2,1,0:T(4,128)S(1)}, f32[6,4,128]{2,1,0:T(4,128)S(1)}, u32[]{:S(2)}, u32[]{:S(2)}) collective-permute-start(f32[6,4,128]{2,1,0:T(4,128)S(1)} %get-tuple-element.18), channel_id=1, source_target_pairs={{17,18},{82,83},{146,147},{210,211},{274,275},{338,339},{402,403},... | collective-permute-start | bytes 36872 | tf_op jit(solution)/shard_map/ppermute | solution.py:503
where the time goes:
time: 62.5 us; the launch traced here: 62.1 us
  starting transfers between devices  54.1 us (87%)
  Pallas kernels  4.72 us (8%)
  waiting for transfers between devices  2.53 us (4%)
  between operations  0.8 us (1%)
    all_to_all x2, starting transfers between devices, exchange(): return lax.all_to_all(rows, EVERY, 0, 0, axis_index_groups=groups)  36.4 us
    ppermute x7, starting transfers between devices, trade(): return lax.ppermute(block, EVERY, pairs)  17.7 us
    pallas_call x4, Pallas kernels, call(): pl.pallas_call(kernel, out_shape=[jax.ShapeDtypeStruct(shape, jnp.float32...  4.72 us
    ppermute x7, waiting for transfers between devices, trade(): return lax.ppermute(block, EVERY, pairs)  2.53 us
  transfers between devices with their start and end apart: 9, of which 1 were waited for; matrix products, arithmetic and copies ran while one was open for 0% of the time, Pallas kernels for 3%

commit v1 on v0

--- a/solution.py
+++ b/solution.py
@@ -140,7 +140,7 @@
     return [half * (b[q] - a[q]) for q in ("r", "m1", "m2", "m3", "e")]
 
 
-def forward_kernel(in_ref, out_ref):
+def forward_kernel(in_ref, _, out_ref):
     row = jnp.max(in_ref[...], axis=0, keepdims=True)
     out_ref[...] = jnp.broadcast_to(row, out_ref.shape)
 
@@ -311,20 +311,50 @@
     sent.wait()
 
 
-def physics_kernel(
+def is_ahead():
+    gx, gy = lax.axis_index("gx"), lax.axis_index("gy")
+    return jnp.logical_and(gy >> 1 < OWN_Y - 1, gx + gy > 0)
+
+
+def ahead_kernel(conserved_ref, raw_ref, xp, xq, xr, xs, yp, yq, out_ref, blend_ref, *scratch):
+    @pl.when(is_ahead())
+    def _():
+        physics(conserved_ref, raw_ref, (xp, xq, xr, xs), (yp, yq), out_ref, blend_ref, *scratch)
+
+
+def rest_kernel(
     conserved_ref,
     raw_ref,
     xp,
     xq,
     xr,
+    xs,
     yp,
     yq,
     yr,
-    xs,
+    done_ref,
+    smooth_ref,
     out_ref,
-    blend_hbm,
     blend_ref,
-    sem,
+    *scratch,
+):
+    @pl.when(is_ahead())
+    def _():
+        out_ref[...] = done_ref[...]
+        blend_ref[...] = smooth_ref[...]
+
+    @pl.when(jnp.logical_not(is_ahead()))
+    def _():
+        physics(conserved_ref, raw_ref, (xp, xq, xr, xs), (yp, yq, yr), out_ref, blend_ref, *scratch)
+
+
+def physics(
+    conserved_ref,
+    raw_ref,
+    x_refs,
+    y_refs,
+    out_ref,
+    blend_ref,
     state_ref,
     xprev_ref,
     xnext_ref,
@@ -333,8 +363,8 @@
 ):
     along_x, along_y = sides()
     for flags, refs, prev_ref, next_ref in (
-        (along_x + along_x[2:], (xp, xq, xr, xs), xprev_ref, xnext_ref),
-        (along_y, (yp, yq, yr), yprev_ref, ynext_ref),
+        (along_x + along_x[2:], x_refs, xprev_ref, xnext_ref),
+        (along_y[: len(y_refs)], y_refs, yprev_ref, ynext_ref),
     ):
         low = high = None
         for flag, ref in zip(flags, refs, strict=True):
@@ -365,8 +395,6 @@
     )
     for element in range(4):
         blend_ref[0, element : element + 1] = compact[4 * element : 4 * element + 1]
-    sent = pltpu.make_async_copy(blend_ref, blend_hbm, sem)
-    sent.start()
     keep = 1.0 - blend
 
     for x in range(4):
@@ -456,10 +484,10 @@
     a, b = load(3), gather(xnext_ref)
     flux, loss = pair_flux(a, b, 0), dissipation(a, b, 0)
     store(3, [(-1.0 / WEIGHTS[3]) * (f - d) for f, d in zip(flux, loss, strict=True)])
-    sent.wait()
-
-
-def scale_kernel(tendency_ref, speed_ref, out_ref):
+
+
+def scale_kernel(tendency_ref, smooth_ref, speed_ref, out_ref, blend_ref):
+    blend_ref[...] = smooth_ref[...]
     row = jnp.max(speed_ref[...], axis=0)
     top = jnp.max(row, axis=1, keepdims=True)
     step = 0.25 / top
@@ -546,27 +574,21 @@
     swap("xP", "yP")
     column = exchange(rows, z_groups())
     swap("xS", "xQ", "yQ", "xR")
-    (forward,) = call(forward_kernel, [(plane, 1, 128)], column)
+    scratch = [
+        pltpu.VMEM((9, 4, 16, 128), jnp.float32),
+        pltpu.VMEM(x_face, jnp.float32),
+        pltpu.VMEM(x_face, jnp.float32),
+        pltpu.VMEM(y_face, jnp.float32),
+        pltpu.VMEM(y_face, jnp.float32),
+    ]
+    results = [(5, 4, 16, 128), (1, 4, 32)]
+    early = [got[name] for name in ("xP", "xQ", "xR", "xS", "yP", "yQ")]
+    ahead = call(ahead_kernel, results, conserved, raw, *early, scratch=scratch)
+    (forward,) = call(forward_kernel, [(plane, 1, 128)], column, ahead[1])
     speeds = exchange(forward, plane_groups())
     swap("yR")
-    tendency, blending = call(
-        physics_kernel,
-        [(5, 4, 16, 128), (1, 4, 32)],
-        conserved,
-        raw,
-        *(got[name] for name in CHAIN_FACES),
-        out_specs=[pl.BlockSpec(memory_space=pltpu.VMEM), pl.BlockSpec(memory_space=pltpu.HBM)],
-        scratch=[
-            pltpu.VMEM((1, 4, 32), jnp.float32),
-            pltpu.SemaphoreType.DMA,
-            pltpu.VMEM((9, 4, 16, 128), jnp.float32),
-            pltpu.VMEM(x_face, jnp.float32),
-            pltpu.VMEM(x_face, jnp.float32),
-            pltpu.VMEM(y_face, jnp.float32),
-            pltpu.VMEM(y_face, jnp.float32),
-        ],
-    )
-    (increment,) = call(scale_kernel, [(5, 4, 16, 128)], tendency, speeds)
+    rest = call(rest_kernel, results, conserved, raw, *early, got["yR"], *ahead, scratch=scratch)
+    increment, blending = call(scale_kernel, results, *rest, speeds)
     return increment, blending
 
 

time: 62.5 us -> 67.8 us (1.085)
  waiting for transfers between devices: 2.53 us -> 8.38 us
    ppermute x7, waiting for transfers between devices: 2.53 us -> 7.14 us  [trade(): return lax.ppermute(block, EVERY, pairs)]
    all_to_all x2, waiting for transfers between devices: 0.01 us -> 1.23 us  [exchange(): return lax.all_to_all(rows, EVERY, 0, 0, axis_index_groups=groups)]
    pallas_call x4 -> x5, Pallas kernels: 4.72 us -> 4.26 us  [call(): pl.pallas_call(kernel, out_shape=[jax.ShapeDtypeStruct(shape, jnp.float32...]
  transfers between devices with their start and end apart: 9 -> 9, of which waited for: 1 -> 3; matrix products, arithmetic and copies ran while one was open for 0% -> 0% of each run, Pallas kernels for 3% -> 1%
where the time goes in v1:
time: 67.8 us; the launch traced here: 67.5 us
  starting transfers between devices  54.1 us (80%)
  waiting for transfers between devices  8.38 us (12%)
  Pallas kernels  4.26 us (6%)
  between operations  0.77 us (1%)
    all_to_all x2, starting transfers between devices, exchange(): return lax.all_to_all(rows, EVERY, 0, 0, axis_index_groups=groups)  36.4 us
    ppermute x7, starting transfers between devices, trade(): return lax.ppermute(block, EVERY, pairs)  17.7 us
    ppermute x7, waiting for transfers between devices, trade(): return lax.ppermute(block, EVERY, pairs)  7.14 us
    pallas_call x5, Pallas kernels, call(): pl.pallas_call(kernel, out_shape=[jax.ShapeDtypeStruct(shape, jnp.float32...  4.26 us
  transfers between devices with their start and end apart: 9, of which 3 were waited for; matrix products, arithmetic and copies ran while one was open for 0% of the time, Pallas kernels for 1%

profile of v1, /device:TPU:1, one launch (start us, length us, event | category | flops | bytes accessed | tf_op | source)
XLA Modules:
  0.0 67.5 jit_solution(5305552548740884545)
XLA Ops:
  0.6 0.0 copy-start
  0.6 1.8 %shard_map.30 = (f32[32,1,128]{2,1,0:T(1,128)}, f32[16,128]{1,0:T(8,128)S(1)}, f32[6,16,128]{2,1,0:T(8,128)S(1)}, f32[6,16,128]{2,1,0:T(8,128)S(1)}, f32[6,16,12...) custom-call(f32[5,4,16,128]{3,2,1,0:T(8,128)} %conserved_ref.3), custom_call_target="tpu_custom_call" | custom-call | tf_op jit(solution)/shard_map/pallas_call | solution.py:500
  2.5 29.5 %all-to-all-start = ((f32[32,1,128]{2,1,0:T(1,128)}), f32[32,1,128]{2,1,0:T(1,128)S(1)}, u32[]{:S(2)}, u32[]{:S(2)}) async-start(f32[32,1,128]{2,1,0:T(1,128)} %get-tuple-element.25), calls=%async_computation | async-start | bytes 32768 | tf_op jit(solution)/shard_map/all_to_all | solution.py:548
  32.0 4.3 %collective-permute-start = (f32[6,16,128]{2,1,0:T(8,128)S(1)}, f32[6,16,128]{2,1,0:T(8,128)S(1)}, u32[]{:S(2)}, u32[]{:S(2)}) collective-permute-start(f32[6,16,128]{2,1,0:T(8,128)S(1)} %get-tuple-element.15), channel_id=1, source_target_pairs={{10,74},{11,75},{12,76},{13,77},{14,78},{15,79},{16,80},{17,81},{6... | collective-permute-start | bytes 147464 | tf_op jit(solution)/shard_map/ppermute | solution.py:531
  36.4 0.7 collective-permute-start.1
  37.1 7.6 %collective-permute-start.3 = (f32[6,16,128]{2,1,0:T(8,128)S(1)}, f32[6,16,128]{2,1,0:T(8,128)S(1)}, u32[]{:S(2)}, u32[]{:S(2)}) collective-permute-start(f32[6,16,128]{2,1,0:T(8,128)S(1)} %get-tuple-element.17), channel_id=1, source_target_pairs={{0,64},{64,0}} | collective-permute-start | bytes 147464 | tf_op jit(solution)/shard_map/ppermute | solution.py:531
  44.6 0.7 collective-permute-start.2
  45.3 1.9 %collective-permute-start.4 = (f32[6,4,128]{2,1,0:T(4,128)S(1)}, f32[6,4,128]{2,1,0:T(4,128)S(1)}, u32[]{:S(2)}, u32[]{:S(2)}) collective-permute-start(f32[6,4,128]{2,1,0:T(4,128)S(1)} %get-tuple-element.18), channel_id=1, source_target_pairs={{64,65},{128,129},{192,193},{256,257},{320,321},{384,385},{448,449... | collective-permute-start | bytes 36872 | tf_op jit(solution)/shard_map/ppermute | solution.py:531
  47.2 2.5 %collective-permute-done.4.yp = f32[6,4,128]{2,1,0:T(4,128)S(1)} collective-permute-done((f32[6,4,128]{2,1,0:T(4,128)S(1)}, f32[6,4,128]{2,1,0:T(4,128)S(1)}, u32[]{:S(2)}, u32[]{:S(2)}) %collective-permute-start.4) | collective-permute-done | bytes 12320 | tf_op jit(solution)/shard_map/ppermute | solution.py:531
  49.7 1.9 %collective-permute-start.5 = (f32[6,4,128]{2,1,0:T(4,128)S(1)}, f32[6,4,128]{2,1,0:T(4,128)S(1)}, u32[]{:S(2)}, u32[]{:S(2)}) collective-permute-start(f32[6,4,128]{2,1,0:T(4,128)S(1)} %get-tuple-element.19), channel_id=1, source_target_pairs={{0,1},{65,66},{129,130},{193,194},{257,258},{321,322},{385,386},{4... | collective-permute-start | bytes 36872 | tf_op jit(solution)/shard_map/ppermute | solution.py:531
  51.6 4.6 %collective-permute-done.5.yq = f32[6,4,128]{2,1,0:T(4,128)S(1)} collective-permute-done((f32[6,4,128]{2,1,0:T(4,128)S(1)}, f32[6,4,128]{2,1,0:T(4,128)S(1)}, u32[]{:S(2)}, u32[]{:S(2)}) %collective-permute-start.5) | collective-permute-done | bytes 12320 | tf_op jit(solution)/shard_map/ppermute | solution.py:531
  56.3 0.0 collective-permute-done.xp
  56.3 0.0 collective-permute-done.1.xq
  56.3 0.0 collective-permute-done.3.xs
  56.3 0.0 collective-permute-done.2.xr
  56.3 0.0 copy-done
  56.3 1.0 %shard_map.31 = (f32[5,4,16,128]{3,2,1,0:T(8,128)S(1)}, f32[1,4,32]{2,1,0:T(4,128)S(1)}) custom-call(f32[5,4,16,128]{3,2,1,0:T(8,128)S(1)} %copy-done, f32[16,128]{1,0:T(8,128)S(1)} %get-tuple-element.14.raw_ref, f32[6,16,128]{2,1,0:T(8,128)S(1)} %collective-permute-done.xp, f32[6,16,128]{2,1,0:T(8,128)S(1)} %collective-permute-done.1.xq, ...), custom_call_target="tpu_custom_call" | custom-call | tf_op jit(solution)/shard_map/pallas_call | solution.py:500
  57.3 0.0 all-to-all-done.in_ref
  57.3 0.6 shard_map.33
  57.9 6.8 %all-to-all-start.1 = ((f32[32,1,128]{2,1,0:T(1,128)}), f32[32,1,128]{2,1,0:T(1,128)S(1)}, u32[]{:S(2)}, u32[]{:S(2)}) async-start(f32[32,1,128]{2,1,0:T(1,128)} %shard_map.33), calls=%async_computation.1 | async-start | bytes 32768 | tf_op jit(solution)/shard_map/all_to_all | solution.py:548
  64.7 0.7 collective-permute-start.6
  65.4 0.0 collective-permute-done.6.yr
  65.5 1.2 %all-to-all-done.1.speed_ref = f32[32,1,128]{2,1,0:T(1,128)S(1)} async-done(((f32[32,1,128]{2,1,0:T(1,128)}), f32[32,1,128]{2,1,0:T(1,128)S(1)}, u32[]{:S(2)}, u32[]{:S(2)}) %all-to-all-start.1) | async-done | bytes 16416 | tf_op jit(solution)/shard_map/all_to_all | solution.py:548
  66.7 0.8 %shard_map.34 = (f32[5,4,16,128]{3,2,1,0:T(8,128)}, f32[1,4,32]{2,1,0:T(4,128)}) custom-call(f32[5,4,16,128]{3,2,1,0:T(8,128)S(1)} %get-tuple-element.23.tendency_ref, f32[1,4,32]{2,1,0:T(4,128)S(1)} %get-tuple-element.24.smooth_ref, f32[32,1,128]{2,1,0:T(1,128)S(1)} %all-to-all-done.1.speed_ref), custom_call_target="tpu_custom_call" | custom-call | tf_op jit(solution)/shard_map/pallas_call | solution.py:500
  (1 shorter events, 0.0 us)
Async XLA Ops:
  0.6 55.7 %copy-start = (f32[5,4,16,128]{3,2,1,0:T(8,128)S(1)}, f32[5,4,16,128]{3,2,1,0:T(8,128)}, u32[]{:S(2)}) copy-start(f32[5,4,16,128]{3,2,1,0:T(8,128)} %conserved_ref.3) | copy-start | bytes 491524
  2.5 54.8 %all-to-all-start = ((f32[32,1,128]{2,1,0:T(1,128)}), f32[32,1,128]{2,1,0:T(1,128)S(1)}, u32[]{:S(2)}, u32[]{:S(2)}) async-start(f32[32,1,128]{2,1,0:T(1,128)} %get-tuple-element.25), calls=%async_computation | async-start | bytes 32768 | tf_op jit(solution)/shard_map/all_to_all | solution.py:548
  32.0 24.2 %collective-permute-start = (f32[6,16,128]{2,1,0:T(8,128)S(1)}, f32[6,16,128]{2,1,0:T(8,128)S(1)}, u32[]{:S(2)}, u32[]{:S(2)}) collective-permute-start(f32[6,16,128]{2,1,0:T(8,128)S(1)} %get-tuple-element.15), channel_id=1, source_target_pairs={{10,74},{11,75},{12,76},{13,77},{14,78},{15,79},{16,80},{17,81},{6... | collective-permute-start | bytes 147464 | tf_op jit(solution)/shard_map/ppermute | solution.py:531
  36.4 19.9 %collective-permute-start.1 = (f32[6,16,128]{2,1,0:T(8,128)S(1)}, f32[6,16,128]{2,1,0:T(8,128)S(1)}, u32[]{:S(2)}, u32[]{:S(2)}) collective-permute-start(f32[6,16,128]{2,1,0:T(8,128)S(1)} %get-tuple-element.16), channel_id=1, source_target_pairs={{1,65},{2,66},{3,67},{4,68},{5,69},{6,70},{7,71},{8,72},{9,73},{74... | collective-permute-start | bytes 147464 | tf_op jit(solution)/shard_map/ppermute | solution.py:531
  37.1 19.2 %collective-permute-start.3 = (f32[6,16,128]{2,1,0:T(8,128)S(1)}, f32[6,16,128]{2,1,0:T(8,128)S(1)}, u32[]{:S(2)}, u32[]{:S(2)}) collective-permute-start(f32[6,16,128]{2,1,0:T(8,128)S(1)} %get-tuple-element.17), channel_id=1, source_target_pairs={{0,64},{64,0}} | collective-permute-start | bytes 147464 | tf_op jit(solution)/shard_map/ppermute | solution.py:531
  44.6 11.7 %collective-permute-start.2 = (f32[6,16,128]{2,1,0:T(8,128)S(1)}, f32[6,16,128]{2,1,0:T(8,128)S(1)}, u32[]{:S(2)}, u32[]{:S(2)}) collective-permute-start(f32[6,16,128]{2,1,0:T(8,128)S(1)} %get-tuple-element.17), channel_id=1, source_target_pairs={{18,82},{19,83},{20,84},{21,85},{22,86},{23,87},{24,88},{25,89},{2... | collective-permute-start | bytes 147464 | tf_op jit(solution)/shard_map/ppermute | solution.py:531
  45.3 4.4 %collective-permute-start.4 = (f32[6,4,128]{2,1,0:T(4,128)S(1)}, f32[6,4,128]{2,1,0:T(4,128)S(1)}, u32[]{:S(2)}, u32[]{:S(2)}) collective-permute-start(f32[6,4,128]{2,1,0:T(4,128)S(1)} %get-tuple-element.18), channel_id=1, source_target_pairs={{64,65},{128,129},{192,193},{256,257},{320,321},{384,385},{448,449... | collective-permute-start | bytes 36872 | tf_op jit(solution)/shard_map/ppermute | solution.py:531
  49.7 6.5 %collective-permute-start.5 = (f32[6,4,128]{2,1,0:T(4,128)S(1)}, f32[6,4,128]{2,1,0:T(4,128)S(1)}, u32[]{:S(2)}, u32[]{:S(2)}) collective-permute-start(f32[6,4,128]{2,1,0:T(4,128)S(1)} %get-tuple-element.19), channel_id=1, source_target_pairs={{0,1},{65,66},{129,130},{193,194},{257,258},{321,322},{385,386},{4... | collective-permute-start | bytes 36872 | tf_op jit(solution)/shard_map/ppermute | solution.py:531
  57.9 8.8 %all-to-all-start.1 = ((f32[32,1,128]{2,1,0:T(1,128)}), f32[32,1,128]{2,1,0:T(1,128)S(1)}, u32[]{:S(2)}, u32[]{:S(2)}) async-start(f32[32,1,128]{2,1,0:T(1,128)} %shard_map.33), calls=%async_computation.1 | async-start | bytes 32768 | tf_op jit(solution)/shard_map/all_to_all | solution.py:548
  64.7 0.7 collective-permute-start.6

commit v2 on v0

--- a/solution.py
+++ b/solution.py
@@ -201,7 +201,7 @@
     return jnp.minimum(raw, 0.5)
 
 
-FIRST_X, MIDDLE_X = 5, 9
+FIRST_X, MIDDLE_X = 4, 9
 MIDDLE_Y = 9
 OWN_Y = 9
 X_TURN = 10
@@ -322,9 +322,7 @@
     yr,
     xs,
     out_ref,
-    blend_hbm,
     blend_ref,
-    sem,
     state_ref,
     xprev_ref,
     xnext_ref,
@@ -365,8 +363,6 @@
     )
     for element in range(4):
         blend_ref[0, element : element + 1] = compact[4 * element : 4 * element + 1]
-    sent = pltpu.make_async_copy(blend_ref, blend_hbm, sem)
-    sent.start()
     keep = 1.0 - blend
 
     for x in range(4):
@@ -456,10 +452,10 @@
     a, b = load(3), gather(xnext_ref)
     flux, loss = pair_flux(a, b, 0), dissipation(a, b, 0)
     store(3, [(-1.0 / WEIGHTS[3]) * (f - d) for f, d in zip(flux, loss, strict=True)])
-    sent.wait()
-
-
-def scale_kernel(tendency_ref, speed_ref, out_ref):
+
+
+def scale_kernel(tendency_ref, smooth_ref, speed_ref, out_ref, blend_ref):
+    blend_ref[...] = smooth_ref[...]
     row = jnp.max(speed_ref[...], axis=0)
     top = jnp.max(row, axis=1, keepdims=True)
     step = 0.25 / top
@@ -549,16 +545,13 @@
     (forward,) = call(forward_kernel, [(plane, 1, 128)], column)
     speeds = exchange(forward, plane_groups())
     swap("yR")
-    tendency, blending = call(
+    tendency, smooth = call(
         physics_kernel,
         [(5, 4, 16, 128), (1, 4, 32)],
         conserved,
         raw,
         *(got[name] for name in CHAIN_FACES),
-        out_specs=[pl.BlockSpec(memory_space=pltpu.VMEM), pl.BlockSpec(memory_space=pltpu.HBM)],
         scratch=[
-            pltpu.VMEM((1, 4, 32), jnp.float32),
-            pltpu.SemaphoreType.DMA,
             pltpu.VMEM((9, 4, 16, 128), jnp.float32),
             pltpu.VMEM(x_face, jnp.float32),
             pltpu.VMEM(x_face, jnp.float32),
@@ -566,7 +559,9 @@
             pltpu.VMEM(y_face, jnp.float32),
         ],
     )
-    (increment,) = call(scale_kernel, [(5, 4, 16, 128)], tendency, speeds)
+    increment, blending = call(
+        scale_kernel, [(5, 4, 16, 128), (1, 4, 32)], tendency, smooth, speeds
+    )
     return increment, blending
 
 

time: 62.5 us -> 62.2 us (level)
  transfers between devices with their start and end apart: 9 -> 9, of which waited for: 1 -> 2; matrix products, arithmetic and copies ran while one was open for 0% -> 0% of each run, Pallas kernels for 3% -> 3%
where the time goes in v2:
time: 62.2 us; the launch traced here: 61.9 us
  starting transfers between devices  54.1 us (87%)
  Pallas kernels  4.22 us (7%)
  waiting for transfers between devices  2.76 us (4%)
  between operations  0.78 us (1%)
    all_to_all x2, starting transfers between devices, exchange(): return lax.all_to_all(rows, EVERY, 0, 0, axis_index_groups=groups)  36.4 us
    ppermute x7, starting transfers between devices, trade(): return lax.ppermute(block, EVERY, pairs)  17.7 us
    pallas_call x4, Pallas kernels, call(): pl.pallas_call(kernel, out_shape=[jax.ShapeDtypeStruct(shape, jnp.float32...  4.22 us
    ppermute x7, waiting for transfers between devices, trade(): return lax.ppermute(block, EVERY, pairs)  2.53 us
  transfers between devices with their start and end apart: 9, of which 2 were waited for; matrix products, arithmetic and copies ran while one was open for 0% of the time, Pallas kernels for 3%

profile of v2, /device:TPU:1, one launch (start us, length us, event | category | flops | bytes accessed | tf_op | source)
XLA Modules:
  0.0 61.9 jit_solution(2050651099561034431)
XLA Ops:
  0.6 0.0 copy-start
  0.6 1.8 %shard_map.30 = (f32[32,1,128]{2,1,0:T(1,128)}, f32[16,128]{1,0:T(8,128)S(1)}, f32[6,16,128]{2,1,0:T(8,128)S(1)}, f32[6,16,128]{2,1,0:T(8,128)S(1)}, f32[6,16,12...) custom-call(f32[5,4,16,128]{3,2,1,0:T(8,128)} %conserved_ref.1), custom_call_target="tpu_custom_call" | custom-call | tf_op jit(solution)/shard_map/pallas_call | solution.py:468
  2.5 29.5 %all-to-all-start = ((f32[32,1,128]{2,1,0:T(1,128)}), f32[32,1,128]{2,1,0:T(1,128)S(1)}, u32[]{:S(2)}, u32[]{:S(2)}) async-start(f32[32,1,128]{2,1,0:T(1,128)} %get-tuple-element.21), calls=%async_computation | async-start | bytes 32768 | tf_op jit(solution)/shard_map/all_to_all | solution.py:516
  32.0 4.3 %collective-permute-start = (f32[6,16,128]{2,1,0:T(8,128)S(1)}, f32[6,16,128]{2,1,0:T(8,128)S(1)}, u32[]{:S(2)}, u32[]{:S(2)}) collective-permute-start(f32[6,16,128]{2,1,0:T(8,128)S(1)} %get-tuple-element.13), channel_id=1, source_target_pairs={{8,72},{9,73},{10,74},{11,75},{12,76},{13,77},{14,78},{15,79},{16,... | collective-permute-start | bytes 147464 | tf_op jit(solution)/shard_map/ppermute | solution.py:499
  36.4 0.7 %collective-permute-start.1 = (f32[6,16,128]{2,1,0:T(8,128)S(1)}, f32[6,16,128]{2,1,0:T(8,128)S(1)}, u32[]{:S(2)}, u32[]{:S(2)}) collective-permute-start(f32[6,16,128]{2,1,0:T(8,128)S(1)} %get-tuple-element.14), channel_id=1, source_target_pairs={{1,65},{2,66},{3,67},{4,68},{5,69},{6,70},{7,71},{72,136},{73,137}... | collective-permute-start | bytes 147464 | tf_op jit(solution)/shard_map/ppermute | solution.py:499
  37.1 7.6 %collective-permute-start.6 = (f32[6,16,128]{2,1,0:T(8,128)S(1)}, f32[6,16,128]{2,1,0:T(8,128)S(1)}, u32[]{:S(2)}, u32[]{:S(2)}) collective-permute-start(f32[6,16,128]{2,1,0:T(8,128)S(1)} %get-tuple-element.15), channel_id=1, source_target_pairs={{0,64},{64,0}} | collective-permute-start | bytes 147464 | tf_op jit(solution)/shard_map/ppermute | solution.py:499
  44.6 0.7 %collective-permute-start.2 = (f32[6,16,128]{2,1,0:T(8,128)S(1)}, f32[6,16,128]{2,1,0:T(8,128)S(1)}, u32[]{:S(2)}, u32[]{:S(2)}) collective-permute-start(f32[6,16,128]{2,1,0:T(8,128)S(1)} %get-tuple-element.15), channel_id=1, source_target_pairs={{18,82},{19,83},{20,84},{21,85},{22,86},{23,87},{24,88},{25,89},{2... | collective-permute-start | bytes 147464 | tf_op jit(solution)/shard_map/ppermute | solution.py:499
  45.3 1.9 %collective-permute-start.3 = (f32[6,4,128]{2,1,0:T(4,128)S(1)}, f32[6,4,128]{2,1,0:T(4,128)S(1)}, u32[]{:S(2)}, u32[]{:S(2)}) collective-permute-start(f32[6,4,128]{2,1,0:T(4,128)S(1)} %get-tuple-element.16), channel_id=1, source_target_pairs={{64,65},{128,129},{192,193},{256,257},{320,321},{384,385},{448,449... | collective-permute-start | bytes 36872 | tf_op jit(solution)/shard_map/ppermute | solution.py:499
  47.2 2.5 %collective-permute-done.3.yp = f32[6,4,128]{2,1,0:T(4,128)S(1)} collective-permute-done((f32[6,4,128]{2,1,0:T(4,128)S(1)}, f32[6,4,128]{2,1,0:T(4,128)S(1)}, u32[]{:S(2)}, u32[]{:S(2)}) %collective-permute-start.3) | collective-permute-done | bytes 12320 | tf_op jit(solution)/shard_map/ppermute | solution.py:499
  49.7 1.9 %collective-permute-start.4 = (f32[6,4,128]{2,1,0:T(4,128)S(1)}, f32[6,4,128]{2,1,0:T(4,128)S(1)}, u32[]{:S(2)}, u32[]{:S(2)}) collective-permute-start(f32[6,4,128]{2,1,0:T(4,128)S(1)} %get-tuple-element.17), channel_id=1, source_target_pairs={{0,1},{65,66},{129,130},{193,194},{257,258},{321,322},{385,386},{4... | collective-permute-start | bytes 36872 | tf_op jit(solution)/shard_map/ppermute | solution.py:499
  51.6 0.0 all-to-all-done.in_ref
  51.7 0.6 %shard_map.32 = f32[32,1,128]{2,1,0:T(1,128)} custom-call(f32[32,1,128]{2,1,0:T(1,128)S(1)} %all-to-all-done.in_ref), custom_call_target="tpu_custom_call" | custom-call | tf_op jit(solution)/shard_map/pallas_call | solution.py:468
  52.3 6.8 %all-to-all-start.1 = ((f32[32,1,128]{2,1,0:T(1,128)}), f32[32,1,128]{2,1,0:T(1,128)S(1)}, u32[]{:S(2)}, u32[]{:S(2)}) async-start(f32[32,1,128]{2,1,0:T(1,128)} %shard_map.32), calls=%async_computation.1 | async-start | bytes 32768 | tf_op jit(solution)/shard_map/all_to_all | solution.py:516
  59.1 0.0 collective-permute-done.4.yq
  59.2 0.7 %collective-permute-start.5 = (f32[6,4,128]{2,1,0:T(4,128)S(1)}, f32[6,4,128]{2,1,0:T(4,128)S(1)}, u32[]{:S(2)}, u32[]{:S(2)}) collective-permute-start(f32[6,4,128]{2,1,0:T(4,128)S(1)} %get-tuple-element.18), channel_id=1, source_target_pairs={{17,18},{82,83},{146,147},{210,211},{274,275},{338,339},{402,403},... | collective-permute-start | bytes 36872 | tf_op jit(solution)/shard_map/ppermute | solution.py:499
  59.8 0.0 collective-permute-done.5.yr
  59.8 0.0 collective-permute-done.xp
  59.8 0.0 collective-permute-done.1.xq
  59.9 0.0 collective-permute-done.6.xs
  59.9 0.0 collective-permute-done.2.xr
  59.9 0.0 copy-done
  59.9 1.0 %shard_map.31 = (f32[5,4,16,128]{3,2,1,0:T(8,128)S(1)}, f32[1,4,32]{2,1,0:T(4,128)S(1)}) custom-call(f32[5,4,16,128]{3,2,1,0:T(8,128)S(1)} %copy-done, f32[16,128]{1,0:T(8,128)S(1)} %get-tuple-element.12.raw_ref, f32[6,16,128]{2,1,0:T(8,128)S(1)} %collective-permute-done.xp, f32[6,16,128]{2,1,0:T(8,128)S(1)} %collective-permute-done.1.xq, ...), custom_call_target="tpu_custom_call" | custom-call | tf_op jit(solution)/shard_map/pallas_call | solution.py:468
  60.9 0.2 all-to-all-done.1.speed_ref
  61.1 0.8 %shard_map.33 = (f32[5,4,16,128]{3,2,1,0:T(8,128)}, f32[1,4,32]{2,1,0:T(4,128)}) custom-call(f32[5,4,16,128]{3,2,1,0:T(8,128)S(1)} %get-tuple-element.19.tendency_ref, f32[1,4,32]{2,1,0:T(4,128)S(1)} %get-tuple-element.20.smooth_ref, f32[32,1,128]{2,1,0:T(1,128)S(1)} %all-to-all-done.1.speed_ref), custom_call_target="tpu_custom_call" | custom-call | tf_op jit(solution)/shard_map/pallas_call | solution.py:468
Async XLA Ops:
  0.6 59.2 %copy-start = (f32[5,4,16,128]{3,2,1,0:T(8,128)S(1)}, f32[5,4,16,128]{3,2,1,0:T(8,128)}, u32[]{:S(2)}) copy-start(f32[5,4,16,128]{3,2,1,0:T(8,128)} %conserved_ref.1) | copy-start | bytes 491524
  2.5 49.2 %all-to-all-start = ((f32[32,1,128]{2,1,0:T(1,128)}), f32[32,1,128]{2,1,0:T(1,128)S(1)}, u32[]{:S(2)}, u32[]{:S(2)}) async-start(f32[32,1,128]{2,1,0:T(1,128)} %get-tuple-element.21), calls=%async_computation | async-start | bytes 32768 | tf_op jit(solution)/shard_map/all_to_all | solution.py:516
  32.0 27.8 %collective-permute-start = (f32[6,16,128]{2,1,0:T(8,128)S(1)}, f32[6,16,128]{2,1,0:T(8,128)S(1)}, u32[]{:S(2)}, u32[]{:S(2)}) collective-permute-start(f32[6,16,128]{2,1,0:T(8,128)S(1)} %get-tuple-element.13), channel_id=1, source_target_pairs={{8,72},{9,73},{10,74},{11,75},{12,76},{13,77},{14,78},{15,79},{16,... | collective-permute-start | bytes 147464 | tf_op jit(solution)/shard_map/ppermute | solution.py:499
  36.4 23.5 %collective-permute-start.1 = (f32[6,16,128]{2,1,0:T(8,128)S(1)}, f32[6,16,128]{2,1,0:T(8,128)S(1)}, u32[]{:S(2)}, u32[]{:S(2)}) collective-permute-start(f32[6,16,128]{2,1,0:T(8,128)S(1)} %get-tuple-element.14), channel_id=1, source_target_pairs={{1,65},{2,66},{3,67},{4,68},{5,69},{6,70},{7,71},{72,136},{73,137}... | collective-permute-start | bytes 147464 | tf_op jit(solution)/shard_map/ppermute | solution.py:499
  37.1 22.8 %collective-permute-start.6 = (f32[6,16,128]{2,1,0:T(8,128)S(1)}, f32[6,16,128]{2,1,0:T(8,128)S(1)}, u32[]{:S(2)}, u32[]{:S(2)}) collective-permute-start(f32[6,16,128]{2,1,0:T(8,128)S(1)} %get-tuple-element.15), channel_id=1, source_target_pairs={{0,64},{64,0}} | collective-permute-start | bytes 147464 | tf_op jit(solution)/shard_map/ppermute | solution.py:499
  44.6 15.2 %collective-permute-start.2 = (f32[6,16,128]{2,1,0:T(8,128)S(1)}, f32[6,16,128]{2,1,0:T(8,128)S(1)}, u32[]{:S(2)}, u32[]{:S(2)}) collective-permute-start(f32[6,16,128]{2,1,0:T(8,128)S(1)} %get-tuple-element.15), channel_id=1, source_target_pairs={{18,82},{19,83},{20,84},{21,85},{22,86},{23,87},{24,88},{25,89},{2... | collective-permute-start | bytes 147464 | tf_op jit(solution)/shard_map/ppermute | solution.py:499
  45.3 4.4 %collective-permute-start.3 = (f32[6,4,128]{2,1,0:T(4,128)S(1)}, f32[6,4,128]{2,1,0:T(4,128)S(1)}, u32[]{:S(2)}, u32[]{:S(2)}) collective-permute-start(f32[6,4,128]{2,1,0:T(4,128)S(1)} %get-tuple-element.16), channel_id=1, source_target_pairs={{64,65},{128,129},{192,193},{256,257},{320,321},{384,385},{448,449... | collective-permute-start | bytes 36872 | tf_op jit(solution)/shard_map/ppermute | solution.py:499
  49.7 9.4 %collective-permute-start.4 = (f32[6,4,128]{2,1,0:T(4,128)S(1)}, f32[6,4,128]{2,1,0:T(4,128)S(1)}, u32[]{:S(2)}, u32[]{:S(2)}) collective-permute-start(f32[6,4,128]{2,1,0:T(4,128)S(1)} %get-tuple-element.17), channel_id=1, source_target_pairs={{0,1},{65,66},{129,130},{193,194},{257,258},{321,322},{385,386},{4... | collective-permute-start | bytes 36872 | tf_op jit(solution)/shard_map/ppermute | solution.py:499
  52.3 8.8 %all-to-all-start.1 = ((f32[32,1,128]{2,1,0:T(1,128)}), f32[32,1,128]{2,1,0:T(1,128)S(1)}, u32[]{:S(2)}, u32[]{:S(2)}) async-start(f32[32,1,128]{2,1,0:T(1,128)} %shard_map.32), calls=%async_computation.1 | async-start | bytes 32768 | tf_op jit(solution)/shard_map/all_to_all | solution.py:516
  59.2 0.7 %collective-permute-start.5 = (f32[6,4,128]{2,1,0:T(4,128)S(1)}, f32[6,4,128]{2,1,0:T(4,128)S(1)}, u32[]{:S(2)}, u32[]{:S(2)}) collective-permute-start(f32[6,4,128]{2,1,0:T(4,128)S(1)} %get-tuple-element.18), channel_id=1, source_target_pairs={{17,18},{82,83},{146,147},{210,211},{274,275},{338,339},{402,403},... | collective-permute-start | bytes 36872 | tf_op jit(solution)/shard_map/ppermute | solution.py:499
